TPU v7x, 32 devices: a whole 2x2x4 slice. The times are simulated.
32 devices in a mesh: row: 8 (over z, x), col: 4 (over y, core).
Axes of the slice: x: 2, y: 2, z: 4, core: 2. Of those that a mesh axis runs over, the one named last changes fastest.
Arguments:
- samples: float32 [4096, 512], P(('row', 'col')), may hold values from -8 to 8
- labels: int32 [4096, 256], P(('row', 'col')), may hold values from -1 to 1, as said below
Outputs:
- statistic: float32 [256], replicated
- proof: float32 [4096], P(('row', 'col'))
- p_value: float32 [], replicated
Inputs may be any that keep to these rules, and one draw needn't show every extreme that they name: `labels`: every column holds exactly 2048 entries +1 and 2048 entries -1.
All inputs are finite; a program needn't handle non-finite values.
Results may differ from a plain program's by a relative error of at most 0.0003.
Values sent between devices are 32-bit elements; how exact they have to be, the bound alone decides.
A program may use at most 64 MiB of HBM per device.

v0:
```python
import functools
import math

import jax
import jax.numpy as jnp
from jax import lax
from jax.experimental import pallas as pl
from jax.experimental.pallas import tpu as pltpu
from jax.sharding import PartitionSpec as P

MESH = pl.DeviceIdType.MESH
F32 = jnp.float32
BF16 = jnp.bfloat16
CHUNKS = 4
PARTS = 2

ROUTES = {1: {}, 2: {0: (1, 1)}, 4: {0: (1, 3), 2: (-1, 1), 3: (-1, 2)}}


def nt(a, b):
    return lax.dot_general(a, b, (((1,), (1,)), ((), ())), preferred_element_type=F32)


def nn(a, b):
    return lax.dot_general(a, b, (((1,), (0,)), ((), ())), preferred_element_type=F32)


def split(v):
    hi = v.astype(BF16)
    return hi, (v - hi.astype(F32)).astype(BF16)


def to_row(column):
    n = column.shape[0]
    return jnp.transpose(jnp.broadcast_to(column, (n, n)))[0:1, :]


class Plan:
    def __init__(self, n_row, n_col, blk, width, perms):
        self.nz = math.gcd(n_row, 4)
        self.nx = n_row // self.nz
        self.nk = math.gcd(n_col, 2)
        self.ny = n_col // self.nk
        self.n_col = n_col
        self.n_lev = self.nx * n_col
        self.blk, self.width, self.perms = blk, width, perms
        self.direct = n_row * n_col <= 32
        self.group = math.gcd(n_col, 4)
        self.rows = blk * n_row * n_col


def kernel(pn, n_send, x_hbm, l_hbm, stat_ref, proof_ref, p_ref, x_ref, l_ref, RX, RL, CX, CL, RHI, RLO, RLB, NR,
           ROWP, PROJ, QUAD, TOT, COLP, S1, R1, S2, R2, in_sem, send, lev_sem, z_sem, s1_send, s1_recv, s2_send, s2_recv, here):
    nx, ny, nz, nk, n_col, n_lev, blk = pn.nx, pn.ny, pn.nz, pn.nk, pn.n_col, pn.n_lev, pn.blk
    row, col = lax.axis_index("row"), lax.axis_index("col")
    z, x = row // nx, row % nx
    y, core = col // nk, col % nk
    me = x * n_col + col
    routes = ROUTES[nz]
    pending = []

    def lev_of(xx, yy, kk):
        return xx * n_col + yy * nk + kk

    def dev(zz, xx, yy, kk):
        return (zz * nx + xx, yy * nk + kk)

    def lev_dev(k):
        return (z * nx + k // n_col, k % n_col)

    loads = [pltpu.make_async_copy(x_hbm, x_ref, in_sem.at[0]), pltpu.make_async_copy(l_hbm, l_ref, in_sem.at[1])]
    for c in loads:
        c.start()
    barrier = pltpu.get_barrier_semaphore()
    for d in range(1, n_lev):
        pl.semaphore_signal(barrier, inc=1, device_id=lev_dev((me + d) % n_lev), device_id_type=MESH)
    for d in range(1, nz):
        pl.semaphore_signal(barrier, inc=1, device_id=dev((z + d) % nz, x, y, core), device_id_type=MESH)
    pl.semaphore_wait(barrier, n_lev - 1 + nz - 1)
    for c in loads:
        c.wait()

    n_dev = nz * n_lev
    direct = pn.direct
    if direct:
        for d in range(1, nz):
            pl.semaphore_signal(here, inc=1, device_id=dev((z + d) % nz, x, y, core), device_id_type=MESH)

    counter = [0]

    def new_sem():
        counter[0] += 1
        return send.at[counter[0] - 1]

    half = blk // PARTS
    piece = blk // CHUNKS

    def lev_copy(k, part, target, own, sem):
        r = pl.ds(part * half, half)
        out = []
        for i, (src, dst) in enumerate(((x_ref, RX), (l_ref, RL))):
            s = src.at[r] if own else dst.at[k, r]
            out.append(pltpu.make_async_remote_copy(
                src_ref=s, dst_ref=dst.at[k, r], send_sem=new_sem() if sem else send.at[0],
                recv_sem=lev_sem.at[k, part * 2 + i], device_id=target, device_id_type=MESH))
        return out

    def lev_send(k, part, target, own=False):
        for c in lev_copy(k, part, target, own, True):
            c.start()
            pending.append(c)

    def lev_wait(k, part):
        for c in lev_copy(k, part, (row, col), False, False):
            c.wait_recv()

    def z_copy(b, ch, target, own, sems):
        r = pl.ds(ch * piece, piece)
        out = []
        for i, (src, dst) in enumerate(((x_ref, CX), (l_ref, CL))):
            s = src.at[r] if own else dst.at[b, r]
            out.append(pltpu.make_async_remote_copy(
                src_ref=s, dst_ref=dst.at[b, r], send_sem=sems[i],
                recv_sem=z_sem.at[b, ch * 2 + i], device_id=target, device_id_type=MESH))
        return out

    z_pending = []

    def z_send(b, ch, at, own):
        sems = [new_sem(), new_sem()]
        to = at + routes[b][0]

        @pl.when(z == at)
        def _():
            for c in z_copy(b, ch, dev(to, x, y, core), own, sems):
                c.start()
        z_pending.append((b, ch, at, own, sems))

    def z_arrive(b, ch, at):
        for c in z_copy(b, ch, (row, col), False, [send.at[0]] * 2):
            c.wait_recv()

    def z_round(hop, ch):
        for b in routes:
            if hop < routes[b][1]:
                at = b + routes[b][0] * hop

                @pl.when(z == at)
                def _():
                    z_arrive(b, ch, at)
                z_send(b, ch, at, False)

    def xm(d):
        return (x + d) % nx

    def ym(d):
        return (y + d) % ny

    other = (core + 1) % nk
    A, B = 0, 1
    for ch in range(CHUNKS):
        for b in routes:
            z_send(b, ch, b, True)
    for d in range(1, nx):
        lev_send(me, A, dev(z, xm(d), y, core), True)
    for d in range(1, ny):
        lev_send(me, B, dev(z, x, ym(d), core), True)
    for d in range(1, nx):
        lev_send(me, B, dev(z, xm(d), y, core), True)
    for d in range(1, ny):
        lev_send(me, A, dev(z, x, ym(d), core), True)
    if nk > 1:
        for part in (A, B):
            lev_send(me, part, dev(z, x, y, other), True)

    def prep(k, xv, lv):
        rows = pl.ds(pl.multiple_of(k * blk, blk), blk)
        hi, lo = split(xv)
        RHI[rows, :] = hi
        RLO[rows, :] = lo
        RLB[rows, :] = lv.astype(F32).astype(BF16)
        NR[:, rows] = to_row(jnp.sum(xv * xv, axis=1, keepdims=True))

    def prep_chunk(xx, skip):
        def step(i, _):
            k = xx * n_col + (col + i) % n_col
            prep(k, RX[k], RL[k])
            return 0

        lax.fori_loop(skip, n_col, step, 0)

    span = pn.group * blk
    scale = -1.0 / (2.0 * pn.width)

    def tile(slot, xx, xv, lv, own):
        chi, clo = split(xv)
        nc = jnp.sum(xv * xv, axis=1, keepdims=True)
        l0 = lv[:, 0:1].astype(F32)
        proj = PROJ[slot]
        tot = TOT[slot:slot + 1, :]
        for j in range(n_col // pn.group):
            base = pl.multiple_of(xx * n_col * blk + j * span, span)
            rows = pl.ds(base, span)
            hi, lo, lb = RHI[rows, :], RLO[rows, :], RLB[rows, :]
            dots = nt(chi, hi) + nt(chi, lo) + nt(clo, hi)
            dist = jnp.maximum(nc + NR[:, rows] - 2.0 * dots, 0.0)
            kern = jnp.exp(dist * scale)
            if own:
                ids = lax.broadcasted_iota(jnp.int32, (blk, span), 1) + base
                mine = lax.broadcasted_iota(jnp.int32, (blk, span), 0) + me * blk
                kern = jnp.where(ids == mine, 0.0, kern)
            kh, kl = split(kern)
            proj = proj + nn(kh, lb) + nn(kl, lb)
            t = jnp.sum(kern, axis=0, keepdims=True)
            for g in range(pn.group):
                tot = tot + t[:, g * blk:(g + 1) * blk]
            if not own:
                ROWP[:, rows] += jnp.sum(kern * l0, axis=0, keepdims=True)
        PROJ[slot] = proj
        TOT[slot:slot + 1, :] = tot

    def line_tiles(hop, chunks, arrive):
        for b in routes:
            if hop <= routes[b][1]:
                at = b + routes[b][0] * hop

                @pl.when(z == at)
                def _():
                    if arrive and hop == routes[b][1]:
                        for ch in range(CHUNKS):
                            z_arrive(b, ch, at)
                    for xx in chunks:
                        tile(b, xx, CX[b], CL[b], False)

    def own_tile(xx):
        tile(nz, xx, x_ref[...], l_ref[...], True)

    prep(me, x_ref[...], l_ref[...])
    ROWP[...] = jnp.zeros_like(ROWP)
    PROJ[...] = jnp.zeros_like(PROJ)
    TOT[...] = jnp.zeros_like(TOT)

    def partner(k, part):
        if nk > 1:
            lev_send(k, part, dev(z, x, y, other))

    z_round(1, 0)
    for d in range(1, nx):
        k = lev_of(xm(d), y, core)
        lev_wait(k, A)
        for e in range(1, ny):
            lev_send(k, A, dev(z, x, ym(e), core))
        partner(k, A)
    for d in range(1, ny):
        k = lev_of(x, ym(d), core)
        lev_wait(k, B)
        for e in range(1, nx):
            lev_send(k, B, dev(z, xm(e), y, core))
        partner(k, B)
    z_round(1, 1)
    z_round(2, 0)
    z_round(1, 2)
    z_round(2, 1)
    z_round(1, 3)
    for d in range(1, ny):
        k = lev_of(x, ym(d), core)
        lev_wait(k, A)
        partner(k, A)
    for d in range(1, nx):
        k = lev_of(xm(d), y, core)
        lev_wait(k, B)
        partner(k, B)
    z_round(2, 2)

    def other_core(xx, ys):
        if nk > 1:
            for e in ys:
                for part in (A, B):
                    lev_wait(lev_of(xx, ym(e), other), part)

    other_core(x, range(ny))
    prep_chunk(x, 1)
    own_tile(x)
    z_round(2, 3)
    line_tiles(1, [x], True)
    for d in range(1, nx):
        for e in range(1, ny):
            k = lev_of(xm(d), ym(e), core)
            for part in (A, B):
                lev_wait(k, part)
                partner(k, part)
    far = [xm(d) for d in range(1, nx)]
    for xx in far:
        other_core(xx, range(ny))
        prep_chunk(xx, 0)
        own_tile(xx)
    line_tiles(1, far, False)
    for hop in range(2, nz):
        line_tiles(hop, [x] + far, True)

    quad = jnp.zeros((1, pn.perms), F32)
    tot = jnp.zeros((1, blk), F32)
    for b in list(routes) + [nz]:
        w = 1.0 if b == nz else 2.0
        lv = l_ref[...] if b == nz else CL[b]
        QUAD[b:b + 1, :] = jnp.zeros((1, pn.perms), F32)
        COLP[b:b + 1, :] = jnp.zeros((1, blk), F32)
        reach = [nz - 1] if b == nz else [b + routes[b][0] * h for h in range(1, routes[b][1] + 1)]

        @pl.when((z >= (0 if b == nz else min(reach))) & (z <= max(reach)))
        def _():
            QUAD[b:b + 1, :] = w * jnp.sum(lv.astype(F32) * PROJ[b], axis=0, keepdims=True)
            COLP[b:b + 1, :] = to_row(PROJ[b][:, 0:1])
        quad = quad + QUAD[b:b + 1, :]
        tot = tot + w * TOT[b:b + 1, :]
    own_proof = COLP[nz:nz + 1, :]

    qr = pn.perms // 128
    if direct:
        def head(ref, i):
            for j in range(qr):
                ref[i, j:j + 1, :] = quad[:, j * 128:(j + 1) * 128]
            ref[i, qr:qr + 1, :] = tot

        index = z * n_lev + me
        none = jnp.zeros((1, 128), F32)
        for k in range(n_lev):
            head(S1, k)
            S1[k, qr + 1:qr + 2, :] = ROWP[:, k * blk:(k + 1) * blk]
        for b in range(nz):
            head(S2, b)
            S2[b, qr + 1:qr + 2, :] = COLP[b:b + 1, :] if b in routes else none
        head(S2, nz)
        S2[nz, qr + 1:qr + 2, :] = none
        if nz > 1:
            pl.semaphore_wait(here, nz - 1)

        def x_copy(dz, d, slot):
            b, k = (z + dz) % nz, (me + d) % n_lev
            src = S1.at[k] if dz == 0 else (S2.at[b] if d == 0 else S2.at[nz])
            return pltpu.make_async_remote_copy(
                src_ref=src, dst_ref=R1.at[slot], send_sem=s1_send.at[dz * n_lev + d], recv_sem=s1_recv.at[slot],
                device_id=(b * nx + k // n_col, k % n_col), device_id_type=MESH)

        pairs = [(dz, d) for dz in reversed(range(nz)) for d in range(n_lev) if dz + d > 0]
        for dz, d in pairs:
            x_copy(dz, d, index).start()
        R1[index] = S1[me]
        for dz, d in pairs:
            x_copy(dz, d, ((z + dz) % nz) * n_lev + (me + d) % n_lev).wait_recv()
        done = R1[0]
        for i in range(1, n_dev):
            done = done + R1[i]
        proof = done[qr + 1:qr + 2, :] + own_proof
    else:
        for k in range(n_lev):
            for i in range(qr):
                S1[k, i:i + 1, :] = quad[:, i * 128:(i + 1) * 128]
            S1[k, qr:qr + 1, :] = tot
            S1[k, qr + 1:qr + 2, :] = ROWP[:, k * blk:(k + 1) * blk]

        def s1_copy(d):
            k = (me + d) % n_lev
            return pltpu.make_async_remote_copy(
                src_ref=S1.at[k], dst_ref=R1.at[me], send_sem=s1_send.at[k], recv_sem=s1_recv.at[me],
                device_id=lev_dev(k), device_id_type=MESH)

        def s1_in(d):
            k = (me + d) % n_lev
            return pltpu.make_async_remote_copy(
                src_ref=S1.at[k], dst_ref=R1.at[k], send_sem=s1_send.at[k], recv_sem=s1_recv.at[k],
                device_id=lev_dev(k), device_id_type=MESH)

        for d in range(1, n_lev):
            s1_copy(d).start()
        acc = S1[me]
        for d in range(1, n_lev):
            s1_in(d).wait_recv()
            acc = acc + R1[(me + d) % n_lev]
        for b in range(nz):
            S2[b, :, :] = acc
            S2[b, qr + 1:qr + 2, :] = COLP[b:b + 1, :] if b in routes else jnp.zeros((1, 128), F32)

        def s2_copy(d):
            b = (z + d) % nz
            return pltpu.make_async_remote_copy(
                src_ref=S2.at[b], dst_ref=R2.at[z], send_sem=s2_send.at[b], recv_sem=s2_recv.at[z],
                device_id=dev(b, x, y, core), device_id_type=MESH)

        def s2_in(d):
            b = (z + d) % nz
            return pltpu.make_async_remote_copy(
                src_ref=S2.at[b], dst_ref=R2.at[b], send_sem=s2_send.at[b], recv_sem=s2_recv.at[b],
                device_id=dev(b, x, y, core), device_id_type=MESH)

        for d in range(1, nz):
            s2_copy(d).start()
        for d in range(1, nz):
            s2_in(d).wait_recv()
        tops = []
        extra = jnp.zeros((1, 128), F32)
        for b in range(nz):
            mine = z == b
            tops.append(jnp.where(mine, acc, R2[b]))
            extra = extra + jnp.where(mine, 0.0, R2[b, qr + 1:qr + 2, :])
        done = functools.reduce(lambda u, v: u + v, tops)
        proof = acc[qr + 1:qr + 2, :] + own_proof + extra
    total = jnp.sum(done[qr:qr + 1, :], axis=1, keepdims=True)
    hf = pn.rows / 2.0
    den = 2.0 * hf * (hf - 1.0)
    stat = total / den + ((2.0 * hf - 1.0) / den) * done[0:qr, :]
    stat_ref[...] = stat
    proof_ref[...] = proof / math.sqrt(pn.rows)
    sg = 1.0 / (1.0 + jnp.exp(-4.0 * (stat - stat[0:1, 0:1])))
    first = (lax.broadcasted_iota(jnp.int32, stat.shape, 0) + lax.broadcasted_iota(jnp.int32, stat.shape, 1)) == 0
    sg = jnp.where(first, 0.0, sg)
    p = jnp.sum(jnp.sum(sg, axis=0, keepdims=True), axis=1, keepdims=True) / (pn.perms - 1)
    p_ref[...] = p

    for c in pending:
        c.wait_send()
    for b, ch, at, own, sems in z_pending:
        @pl.when(z == at)
        def _():
            for c in z_copy(b, ch, dev(at + routes[b][0], x, y, core), own, sems):
                c.wait_send()
    if direct:
        for dz, d in pairs:
            x_copy(dz, d, index).wait_send()
    else:
        for d in range(1, n_lev):
            s1_copy(d).wait_send()
        for d in range(1, nz):
            s2_copy(d).wait_send()
    assert counter[0] == n_send


def send_count(pn):
    nx, ny, nk, nz = pn.nx, pn.ny, pn.nk, pn.nz
    own = 2 * (nx - 1) + 2 * (ny - 1) + (2 if nk > 1 else 0)
    fwd = 2 * (nx - 1) * (ny - 1)
    core = 2 * (nx * ny - 1) if nk > 1 else 0
    line = sum(h for _, h in ROUTES[nz].values()) * CHUNKS
    return 2 * (own + fwd + core + line)


def solution(mesh):
    n_row, n_col = mesh.shape["row"], mesh.shape["col"]

    def shards(samples, labels):
        blk, width = samples.shape
        perms = labels.shape[1]
        pn = Plan(n_row, n_col, blk, width, perms)
        n_send = send_count(pn)
        n_lev, nz = pn.n_lev, pn.nz
        msg = perms // 128 + 2
        slots = n_row * n_col if pn.direct else n_lev
        vm = pl.BlockSpec(memory_space=pltpu.VMEM)
        hbm = pl.BlockSpec(memory_space=pl.ANY)
        dma = pltpu.SemaphoreType.DMA
        stat, proof, p = pl.pallas_call(
            functools.partial(kernel, pn, n_send),
            out_shape=(
                jax.ShapeDtypeStruct((perms // 128, 128), F32),
                jax.ShapeDtypeStruct((1, blk), F32),
                jax.ShapeDtypeStruct((1, 1), F32),
            ),
            in_specs=[hbm, hbm],
            out_specs=(vm, vm, vm),
            scratch_shapes=[
                pltpu.VMEM((blk, width), F32),
                pltpu.VMEM((blk, perms), jnp.int32),
                pltpu.VMEM((n_lev, blk, width), F32),
                pltpu.VMEM((n_lev, blk, perms), jnp.int32),
                pltpu.VMEM((nz, blk, width), F32),
                pltpu.VMEM((nz, blk, perms), jnp.int32),
                pltpu.VMEM((n_lev * blk, width), BF16),
                pltpu.VMEM((n_lev * blk, width), BF16),
                pltpu.VMEM((n_lev * blk, perms), BF16),
                pltpu.VMEM((1, n_lev * blk), F32),
                pltpu.VMEM((1, n_lev * blk), F32),
                pltpu.VMEM((nz + 1, blk, perms), F32),
                pltpu.VMEM((nz + 1, perms), F32),
                pltpu.VMEM((nz + 1, blk), F32),
                pltpu.VMEM((nz + 1, blk), F32),
                pltpu.VMEM((n_lev, msg, 128), F32),
                pltpu.VMEM((slots, msg, 128), F32),
                pltpu.VMEM((nz + 1, msg, 128), F32),
                pltpu.VMEM((nz, msg, 128), F32),
                dma((2,)),
                dma((n_send,)),
                dma((n_lev, 2 * PARTS)),
                dma((nz, 2 * CHUNKS)),
                dma((slots,)),
                dma((slots,)),
                dma((nz,)),
                dma((nz,)),
                pltpu.SemaphoreType.REGULAR,
            ],
            compiler_params=pltpu.CompilerParams(
                collective_id=0, has_side_effects=True, vmem_limit_bytes=60 * 1024 * 1024
            ),
        )(samples, labels)
        return stat.reshape(perms), proof.reshape(blk), p.reshape(())

    placed = (P(("row", "col"), None), P(("row", "col"), None))
    return jax.shard_map(
        shards, mesh=mesh, in_specs=placed, out_specs=(P(), P(("row", "col")), P()), check_vma=False
    )
```

profile of v0, /device:TPU:0, one launch (start us, length us, event | category | flops | bytes accessed | tf_op | source)
XLA Modules:
  0.0 38.6 jit_solution(17229138267163226869)
XLA Ops:
  0.6 34.4 %shard_map.49 = (f32[2,128]{1,0:T(2,128)}, f32[1,128]{1,0:T(1,128)}, f32[1,1]{1,0:T(1,128)}) custom-call(f32[128,512]{1,0:T(8,128)} %x_hbm.1, s32[128,256]{1,0:T(8,128)} %l_hbm.1), custom_call_target="tpu_custom_call" | custom-call | tf_op jit(solution)/shard_map/pallas_call | solution.py:461
  35.1 0.0 copy-start
  35.1 0.7 %copy-done = f32[2,128]{1,0:T(2,128)S(1)} copy-done((f32[2,128]{1,0:T(2,128)S(1)}, f32[2,128]{1,0:T(2,128)}, u32[]{:S(2)}) %copy-start) | copy-done | bytes 1048
  35.7 0.0 copy-start.1
  35.7 0.6 %copy.8 = f32[256]{0:T(256)} copy(f32[256]{0:T(256)S(1)} %bitcast.3) | data formatting | bytes 2048
  36.3 0.1 copy-done.1
  36.4 0.5 %copy.9 = f32[128]{0:T(128)} copy(f32[128]{0:T(128)S(1)} %bitcast.4) | data formatting | bytes 1024
Async XLA Ops:
  35.1 0.7 %copy-start = (f32[2,128]{1,0:T(2,128)S(1)}, f32[2,128]{1,0:T(2,128)}, u32[]{:S(2)}) copy-start(f32[2,128]{1,0:T(2,128)} %get-tuple-element.6) | copy-start | bytes 3076
  35.7 0.6 %copy-start.1 = (f32[1,128]{1,0:T(1,128)S(1)}, f32[1,128]{1,0:T(1,128)}, u32[]{:S(2)}) copy-start(f32[1,128]{1,0:T(1,128)} %get-tuple-element.7) | copy-start | bytes 1540
where the time goes:
time: 38.8 us; the launch traced here: 38.6 us
  Pallas kernels  34.4 us (89%)
  between operations  2.4 us (6%)
  local copies, waits for them, and re-layouts  1.8 us (5%)
    pallas_call x1, Pallas kernels, shards(): pl.pallas_call(functools.partial(kernel, pn, n_send), out_shape=(jax.Shap...  34.4 us
    unnamed x6, local copies, waits for them, and re-layouts  1.8 us

commit v1 on v0

--- a/solution.py
+++ b/solution.py
@@ -13,6 +13,7 @@
 BF16 = jnp.bfloat16
 CHUNKS = 4
 PARTS = 2
+LIMIT = 60 * 1024 * 1024
 
 ROUTES = {1: {}, 2: {0: (1, 1)}, 4: {0: (1, 3), 2: (-1, 1), 3: (-1, 2)}}
 
@@ -444,6 +445,459 @@
     return 2 * (own + fwd + core + line)
 
 
+def line_kernel(x_hbm, l_hbm, out_ref, x_ref, l_ref, GX, GL, CX, CL, CC, HI, LO, LB, NR, NC, L0, OWN0,
+                ROWP, PROJ, TOT, S1, S2, R1, in_sem, xy_send, xy_recv, z_send, z_recv, m_send, m_recv, line, here):
+    blk, width = x_ref.shape
+    perms = l_ref.shape[1]
+    nx, ny, nk, nz, n_lev = 2, 2, 2, 4, 8
+    row, col = lax.axis_index("row"), lax.axis_index("col")
+    z, x = row // nx, row % nx
+    y, core = col // nk, col % nk
+    qr = perms // 128
+    OWN = 4
+    A, B = 0, 1
+
+    def dev(zz, xx, yy, kk):
+        return (zz * nx + xx, yy * nk + kk)
+
+    def signal(sem, to):
+        pl.semaphore_signal(sem, inc=1, device_id=to, device_id_type=MESH)
+
+    def remote(src, dst, ss, rs, to):
+        return pltpu.make_async_remote_copy(src_ref=src, dst_ref=dst, send_sem=ss, recv_sem=rs, device_id=to,
+                                            device_id_type=MESH)
+
+    here_dev = (row, col)
+    x_dev, y_dev, k_dev = dev(z, 1 - x, y, core), dev(z, x, 1 - y, core), dev(z, x, y, 1 - core)
+    place = [(xx, yy, kk) for xx, yy, kk in ((x, y, core), (x, y, 1 - core), (1 - x, y, core), (x, 1 - y, core),
+             (1 - x, y, 1 - core), (x, 1 - y, 1 - core), (1 - x, 1 - y, core), (1 - x, 1 - y, 1 - core))]
+
+    loads = [pltpu.make_async_copy(x_hbm, x_ref, in_sem.at[0]), pltpu.make_async_copy(l_hbm, l_ref, in_sem.at[1])]
+    for c in loads:
+        c.start()
+    barrier = pltpu.get_barrier_semaphore()
+    for to in (x_dev, y_dev, k_dev):
+        signal(barrier, to)
+
+    @pl.when(z > 0)
+    def _():
+        signal(barrier, dev(z - 1, x, y, core))
+
+    @pl.when(z < nz - 1)
+    def _():
+        signal(barrier, dev(z + 1, x, y, core))
+
+    ROWP[...] = jnp.zeros_like(ROWP)
+    PROJ[...] = jnp.zeros_like(PROJ)
+    TOT[...] = jnp.zeros_like(TOT)
+    for c in reversed(loads):
+        c.wait()
+    OWN0[...] = to_row(l_ref[:, 0:1].astype(F32)).astype(jnp.int32)
+    pl.semaphore_wait(barrier, 3 + jnp.where(z > 0, 1, 0) + jnp.where(z < nz - 1, 1, 0))
+
+    half = blk // 2
+
+    def xy_copy(src, dst, part, i, to):
+        r = pl.ds(part * half, half)
+        mine, buf = ((x_ref, GX), (l_ref, GL))[i]
+        s = mine.at[r] if src == 0 else buf.at[src, r]
+        n = part * 2 + i
+        return remote(s, buf.at[dst, r], xy_send.at[dst, n], xy_recv.at[dst, n], to)
+
+    sent = []
+    X, L = 0, 1
+
+    def xy_start(src, dst, part, to, kinds=(X, L)):
+        for i in kinds:
+            c = xy_copy(src, dst, part, i, to)
+            c.start()
+            sent.append(c)
+
+    def xy_wait(at, parts=(A, B), kinds=(X, L)):
+        for part in parts:
+            for i in kinds:
+                xy_copy(at, at, part, i, here_dev).wait_recv()
+
+    piece = blk // 4
+    SAM, LAB = [0, 1, 2, 3], [5, 6, 7, 8]
+
+    def z_copy(b, p, own, to):
+        if p == 4:
+            src, dst = (OWN0 if own else CC.at[b]), CC.at[b]
+        else:
+            r = pl.ds((p if p < 4 else p - 5) * piece, piece)
+            mine, buf = (x_ref, CX) if p < 4 else (l_ref, CL)
+            src, dst = (mine.at[r] if own else buf.at[b, r]), buf.at[b, r]
+        return remote(src, dst, z_send.at[b, p], z_recv.at[b, p], to)
+
+    def z_start(b, ps, own, step):
+        for p in ps:
+            z_copy(b, p, own, dev(z + step, x, y, core)).start()
+
+    def z_wait(b, ps):
+        for p in ps:
+            z_copy(b, p, False, here_dev).wait_recv()
+
+    def z_pass(b, ps, step):
+        for p in ps:
+            z_wait(b, [p])
+            z_start(b, [p], False, step)
+
+    def at_z(*levels):
+        cond = z == levels[0]
+        for v in levels[1:]:
+            cond = cond | (z == v)
+        return pl.when(cond)
+
+    @at_z(0)
+    def _():
+        z_start(0, SAM + [4] + LAB, True, 1)
+
+    @at_z(2)
+    def _():
+        z_start(2, SAM + [4], True, -1)
+        signal(line, dev(1, x, y, core))
+
+    @at_z(3)
+    def _():
+        z_start(3, SAM + [4] + LAB, True, -1)
+
+    @at_z(1)
+    def _():
+        signal(line, dev(2, x, y, core))
+
+    xy_start(0, 2, A, x_dev)
+    xy_start(0, 3, B, y_dev)
+    xy_start(0, 2, B, x_dev)
+    xy_start(0, 3, A, y_dev)
+    xy_start(0, 1, A, k_dev)
+    xy_start(0, 1, B, k_dev)
+
+    scale = -1.0 / (2.0 * width)
+    span = nk * blk
+
+    def put(at, v):
+        hi, lo = split(v)
+        rows = slice(at, at + blk)
+        HI[rows, :] = hi
+        LO[rows, :] = lo
+        return jnp.sum(v * v, axis=1, keepdims=True)
+
+    def prep(at, v, lv):
+        n = put(at * blk, v)
+        rows = slice(at * blk, (at + 1) * blk)
+        LB[rows, :] = lv.astype(F32).astype(BF16)
+        NR[:, rows] = to_row(n)
+        return n
+
+    def prep_at(at):
+        prep(at, GX[at], GL[at])
+
+    def prep_line(b):
+        NC[b] = put((n_lev + b) * blk, CX[b])
+        L0[b] = jnp.transpose(jnp.broadcast_to(CC[b], (blk, blk)))[:, 0:1].astype(F32)
+
+    def slot_of(j):
+        return jnp.where(j == 0, OWN, jnp.where(j == 1, jnp.where(z == 2, 3, 0),
+                         jnp.where(j == 2, jnp.where(z == 1, 2, 0), 3)))
+
+    def unit(j, g):
+        s = slot_of(j)
+        own = s == OWN
+        c = pl.ds(pl.multiple_of(jnp.where(own, 0, n_lev + s) * blk, blk), blk)
+        rows = pl.ds(pl.multiple_of(g * span, span), span)
+        chi, clo = HI[c, :], LO[c, :]
+        hi, lo, lb = HI[rows, :], LO[rows, :], LB[rows, :]
+        dots = nt(chi, hi) + nt(chi, lo) + nt(clo, hi)
+        dist = jnp.maximum(NC[s] + NR[:, rows] - 2.0 * dots, 0.0)
+        kern = jnp.exp(dist * scale)
+        gap = lax.broadcasted_iota(jnp.int32, kern.shape, 1) - lax.broadcasted_iota(jnp.int32, kern.shape, 0)
+        kern = jnp.where(gap == jnp.where(own & (g == 0), 0, n_lev * blk), 0.0, kern)
+        kh, kl = split(kern)
+        PROJ[s] += nn(kh, lb) + nn(kl, lb)
+        t = jnp.sum(kern, axis=0, keepdims=True)
+        w = jnp.where(own, 1.0, 2.0)
+        TOT[...] += w * (t[:, :blk] + t[:, blk:])
+        ROWP[:, rows] += jnp.sum(kern * L0[s], axis=0, keepdims=True)
+
+    def units(j0, j1, g0, g1):
+        def outer(j, _):
+            def inner(g, _):
+                unit(j, g)
+                return 0
+            lax.fori_loop(g0, g1, inner, 0)
+            return 0
+        lax.fori_loop(j0, j1, outer, 0)
+
+    early = jnp.where(z == 0, 1, 4 - z)
+    every = jnp.where(z == 0, 1, 5 - z)
+    NC[OWN] = prep(0, x_ref[...], l_ref[...])
+    L0[OWN] = jnp.zeros((blk, 1), F32)
+    xy_wait(1)
+    prep_at(1)
+    units(0, 1, 0, 1)
+
+    @at_z(1)
+    def _():
+        z_pass(0, [0, 1], 1)
+        pl.semaphore_wait(line, 1)
+        signal(line, dev(0, x, y, core))
+        z_pass(0, [2], 1)
+
+    @at_z(2)
+    def _():
+        z_pass(3, [0, 1], -1)
+        pl.semaphore_wait(line, 1)
+        signal(line, dev(3, x, y, core))
+        z_pass(3, [2], -1)
+
+    xy_wait(2, (A,))
+    xy_start(2, 6, A, y_dev)
+    xy_start(2, 4, A, k_dev)
+    xy_wait(3, (B,))
+    xy_start(3, 6, B, x_dev)
+    xy_start(3, 5, B, k_dev)
+
+    @at_z(1)
+    def _():
+        z_pass(0, [3, 4], 1)
+        prep_line(0)
+        z_wait(2, SAM + [4])
+        prep_line(2)
+
+    @at_z(2)
+    def _():
+        z_pass(3, [3, 4], -1)
+        z_start(2, LAB, True, -1)
+        prep_line(3)
+        z_pass(0, [0], 1)
+
+    units(1, early, 0, 1)
+
+    @at_z(1)
+    def _():
+        z_pass(0, LAB, 1)
+
+    @at_z(2)
+    def _():
+        z_pass(0, [1], 1)
+        z_pass(3, LAB[:3], -1)
+        z_pass(0, [2], 1)
+        z_pass(3, LAB[3:], -1)
+
+    xy_wait(2, (B,))
+    xy_start(2, 4, B, k_dev)
+    xy_wait(3, (A,))
+    xy_start(3, 5, A, k_dev)
+    prep_at(2)
+    prep_at(3)
+    units(0, early, 1, 2)
+
+    @at_z(2)
+    def _():
+        z_pass(0, [3, 4], 1)
+        prep_line(0)
+
+    xy_wait(4)
+    xy_wait(5)
+    prep_at(4)
+    prep_at(5)
+    units(0, early, 2, 3)
+
+    @at_z(2)
+    def _():
+        z_pass(0, LAB[:2], 1)
+
+    for part in (A, B):
+        xy_wait(6, (part,), (X,))
+        xy_start(6, 7, part, k_dev, (X,))
+
+    @at_z(1)
+    def _():
+        z_wait(3, SAM + [4])
+        prep_line(3)
+
+    @at_z(1, 2)
+    def _():
+        units(early, every, 0, 1)
+
+    for part in (A, B):
+        xy_wait(6, (part,), (L,))
+        xy_start(6, 7, part, k_dev, (L,))
+
+    @at_z(2)
+    def _():
+        z_pass(0, LAB[2:], 1)
+
+    @at_z(3)
+    def _():
+        z_wait(0, SAM + [4])
+        prep_line(0)
+
+    @at_z(0, 3)
+    def _():
+        pl.semaphore_wait(line, 1)
+
+    units(early, every, jnp.where(z == 3, 0, 1), 3)
+    prep_at(6)
+    xy_wait(7)
+    for xx, yy, kk in place[1:]:
+        signal(here, dev(z, xx, yy, kk))
+    prep_at(7)
+    units(0, every, 3, 4)
+
+    none = jnp.zeros((1, 128), F32)
+    own_proof = to_row(PROJ[OWN][:, 0:1])
+    tot = TOT[...]
+    for i in range(n_lev):
+        S1[i, qr:qr + 1, :] = tot
+        S1[i, qr + 1:qr + 2, :] = ROWP[:, i * blk:(i + 1) * blk]
+    for b in range(nz + 1):
+        S2[b, qr:qr + 1, :] = tot
+        S2[b, qr + 1:qr + 2, :] = to_row(PROJ[b][:, 0:1]) if b in (0, 2, 3) else none
+
+    def quad_of(s, lv):
+        return jnp.sum(lv.astype(F32) * PROJ[s], axis=0, keepdims=True)
+
+    def add(q):
+        for j in range(qr):
+            S2[nz, j:j + 1, :] += q[:, j * 128:(j + 1) * 128]
+
+    S2[nz, 0:qr, :] = jnp.zeros((qr, 128), F32)
+    add(quad_of(OWN, l_ref[...]))
+
+    @at_z(3)
+    def _():
+        z_wait(0, LAB)
+
+    @at_z(1, 2, 3)
+    def _():
+        add(2.0 * quad_of(0, CL[0]))
+
+    @at_z(1)
+    def _():
+        z_wait(2, LAB)
+        add(2.0 * quad_of(2, CL[2]))
+        z_wait(3, LAB)
+
+    @at_z(1, 2)
+    def _():
+        add(2.0 * quad_of(3, CL[3]))
+
+    q = S2[nz, 0:qr, :]
+    for i in range(n_lev):
+        S1[i, 0:qr, :] = q
+    for b in range(nz):
+        S2[b, 0:qr, :] = q
+    index = z * n_lev + x * 4 + col
+    pl.semaphore_wait(here, n_lev - 1)
+
+    def m_copy(dz, i, incoming):
+        b = (z + dz) % nz
+        xx, yy, kk = place[i]
+        src = S1.at[i] if dz == 0 else (S2.at[b] if i == 0 else S2.at[nz])
+        slot = b * n_lev + xx * 4 + yy * nk + kk if incoming else index
+        return remote(src, R1.at[slot], m_send.at[dz * n_lev + i], m_recv.at[slot], dev(b, xx, yy, kk))
+
+    pairs = [(dz, i) for dz in reversed(range(nz)) for i in range(n_lev) if dz + i > 0]
+    for dz, i in pairs:
+        m_copy(dz, i, False).start()
+    R1[index] = S1[0]
+    for dz, i in pairs:
+        m_copy(dz, i, True).wait_recv()
+    done = R1[0]
+    for i in range(1, nz * n_lev):
+        done = done + R1[i]
+    out_ref[0:qr + 1, :] = done[0:qr + 1, :]
+    out_ref[qr + 1:qr + 2, :] = done[qr + 1:qr + 2, :] + own_proof
+
+    for c in sent:
+        c.wait_send()
+    for at, b in ((0, 0), (1, 0), (2, 0), (2, 2), (2, 3), (3, 3)):
+        @at_z(at)
+        def _():
+            for p in SAM + [4] + LAB:
+                z_copy(b, p, False, here_dev).wait_send()
+    for dz, i in pairs:
+        m_copy(dz, i, False).wait_send()
+
+
+def finish(rows, perms, r_ref, stat_ref, proof_ref, p_ref):
+    qr = perms // 128
+    total = jnp.sum(r_ref[qr:qr + 1, :], axis=1, keepdims=True)
+    hf = rows / 2.0
+    den = 2.0 * hf * (hf - 1.0)
+    stat = total / den + ((2.0 * hf - 1.0) / den) * r_ref[0:qr, :]
+    stat_ref[...] = stat
+    proof_ref[...] = r_ref[qr + 1:qr + 2, :] / math.sqrt(rows)
+    sg = 1.0 / (1.0 + jnp.exp(-4.0 * (stat - stat[0:1, 0:1])))
+    first = (lax.broadcasted_iota(jnp.int32, stat.shape, 0) + lax.broadcasted_iota(jnp.int32, stat.shape, 1)) == 0
+    sg = jnp.where(first, 0.0, sg)
+    p_ref[...] = jnp.sum(jnp.sum(sg, axis=0, keepdims=True), axis=1, keepdims=True) / (perms - 1)
+
+
+def line_call(samples, labels):
+    blk, width = samples.shape
+    perms = labels.shape[1]
+    qr = perms // 128
+    nz, n_lev = 4, 8
+    slots = nz * n_lev
+    i32 = jnp.int32
+    dma = pltpu.SemaphoreType.DMA
+    vm = pl.BlockSpec(memory_space=pltpu.VMEM)
+    hbm = pl.BlockSpec(memory_space=pl.ANY)
+    res = pl.pallas_call(
+        line_kernel,
+        out_shape=jax.ShapeDtypeStruct((qr + 2, 128), F32),
+        in_specs=[hbm, hbm],
+        out_specs=vm,
+        scratch_shapes=[
+            pltpu.VMEM((blk, width), F32),
+            pltpu.VMEM((blk, perms), i32),
+            pltpu.VMEM((n_lev, blk, width), F32),
+            pltpu.VMEM((n_lev, blk, perms), i32),
+            pltpu.VMEM((nz, blk, width), F32),
+            pltpu.VMEM((nz, blk, perms), i32),
+            pltpu.VMEM((nz, 1, blk), i32),
+            pltpu.VMEM(((n_lev + nz) * blk, width), BF16),
+            pltpu.VMEM(((n_lev + nz) * blk, width), BF16),
+            pltpu.VMEM((n_lev * blk, perms), BF16),
+            pltpu.VMEM((1, n_lev * blk), F32),
+            pltpu.VMEM((nz + 1, blk, 1), F32),
+            pltpu.VMEM((nz + 1, blk, 1), F32),
+            pltpu.VMEM((1, blk), i32),
+            pltpu.VMEM((1, n_lev * blk), F32),
+            pltpu.VMEM((nz + 1, blk, perms), F32),
+            pltpu.VMEM((1, blk), F32),
+            pltpu.VMEM((n_lev, qr + 2, 128), F32),
+            pltpu.VMEM((nz + 1, qr + 2, 128), F32),
+            pltpu.VMEM((slots, qr + 2, 128), F32),
+            dma((2,)),
+            dma((n_lev, 4)),
+            dma((n_lev, 4)),
+            dma((nz, 9)),
+            dma((nz, 9)),
+            dma((slots,)),
+            dma((slots,)),
+            pltpu.SemaphoreType.REGULAR,
+            pltpu.SemaphoreType.REGULAR,
+        ],
+        compiler_params=pltpu.CompilerParams(
+            collective_id=1, has_side_effects=True, vmem_limit_bytes=LIMIT
+        ),
+    )(samples, labels)
+    return pl.pallas_call(
+        functools.partial(finish, blk * slots, perms),
+        out_shape=(
+            jax.ShapeDtypeStruct((qr, 128), F32),
+            jax.ShapeDtypeStruct((1, blk), F32),
+            jax.ShapeDtypeStruct((1, 1), F32),
+        ),
+        in_specs=[vm],
+        out_specs=(vm, vm, vm),
+    )(res)
+
+
 def solution(mesh):
     n_row, n_col = mesh.shape["row"], mesh.shape["col"]
 
@@ -453,6 +907,9 @@
         pn = Plan(n_row, n_col, blk, width, perms)
         n_send = send_count(pn)
         n_lev, nz = pn.n_lev, pn.nz
+        if (pn.nx, pn.ny, pn.nk, nz, blk) == (2, 2, 2, 4, 128):
+            stat, proof, p = line_call(samples, labels)
+            return stat.reshape(perms), proof.reshape(blk), p.reshape(())
         msg = perms // 128 + 2
         slots = n_row * n_col if pn.direct else n_lev
         vm = pl.BlockSpec(memory_space=pltpu.VMEM)

time: 38.8 us -> 34.2 us (0.88)
  local copies, waits for them, and re-layouts: 1.8 us -> 0 us
  between operations: 2.4 us -> 0.64 us
  Pallas kernels: 34.4 us -> 33.4 us
    unnamed x6 -> x0, local copies, waits for them, and re-layouts: 1.8 us -> none
    pallas_call x1 -> x2, Pallas kernels: 34.4 us -> 33.4 us  [the longest x1 32 us: line_call(): pl.pallas_call(line_kernel, out_shape=jax.ShapeDtypeStruct((qr + 2, 128),...]
where the time goes in v1:
time: 34.2 us; the launch traced here: 34.1 us
  Pallas kernels  33.4 us (98%)
  between operations  0.64 us (2%)
    pallas_call x1, Pallas kernels, line_call(): pl.pallas_call(line_kernel, out_shape=jax.ShapeDtypeStruct((qr + 2, 128),...  32 us
    pallas_call x1, Pallas kernels, line_call(): pl.pallas_call(functools.partial(finish, blk * slots, perms), out_shape=(...  1.4 us

profile of v1, /device:TPU:0, one launch (start us, length us, event | category | flops | bytes accessed | tf_op | source)
XLA Modules:
  0.0 34.1 jit_solution(13416088475721162093)
XLA Ops:
  0.6 32.0 %shard_map.49.r_ref = f32[4,128]{1,0:T(4,128)} custom-call(f32[128,512]{1,0:T(8,128)} %x_hbm.1, s32[128,256]{1,0:T(8,128)} %l_hbm.1), custom_call_target="tpu_custom_call" | custom-call | tf_op jit(solution)/shard_map/pallas_call | solution.py:849
  32.7 1.4 %shard_map.50 = (f32[2,128]{1,0:T(2,128)}, f32[1,128]{1,0:T(1,128)}, f32[1,1]{1,0:T(1,128)}) custom-call(f32[4,128]{1,0:T(4,128)} %shard_map.49.r_ref), custom_call_target="tpu_custom_call" | custom-call | tf_op jit(solution)/shard_map/pallas_call | solution.py:889

commit v2 on v1

--- a/solution.py
+++ b/solution.py
@@ -445,7 +445,7 @@
     return 2 * (own + fwd + core + line)
 
 
-def line_kernel(x_hbm, l_hbm, out_ref, x_ref, l_ref, GX, GL, CX, CL, CC, HI, LO, LB, NR, NC, L0, OWN0,
+def line_kernel(x_hbm, l_hbm, out_ref, x_ref, l_ref, GX, GL, CX, CL, CC, HI, LO, LB, SH, SL, NR, NC, L0, OWN0,
                 ROWP, PROJ, TOT, S1, S2, R1, in_sem, xy_send, xy_recv, z_send, z_recv, m_send, m_recv, line, here):
     blk, width = x_ref.shape
     perms = l_ref.shape[1]
@@ -454,7 +454,6 @@
     z, x = row // nx, row % nx
     y, core = col // nk, col % nk
     qr = perms // 128
-    OWN = 4
     A, B = 0, 1
 
     def dev(zz, xx, yy, kk):
@@ -576,66 +575,73 @@
     scale = -1.0 / (2.0 * width)
     span = nk * blk
 
-    def put(at, v):
+    order = {0: [], 1: [0, 2, 3], 2: [3, 0], 3: [0]}
+
+    def norms(v):
+        return jnp.sum(v * v, axis=1, keepdims=True)
+
+    def prep(at, v, lv):
         hi, lo = split(v)
-        rows = slice(at, at + blk)
+        n = norms(v)
+        rows = slice(at * blk, (at + 1) * blk)
         HI[rows, :] = hi
         LO[rows, :] = lo
-        return jnp.sum(v * v, axis=1, keepdims=True)
-
-    def prep(at, v, lv):
-        n = put(at * blk, v)
-        rows = slice(at * blk, (at + 1) * blk)
         LB[rows, :] = lv.astype(F32).astype(BF16)
         NR[:, rows] = to_row(n)
-        return n
+        if at == 0:
+            SH[rows, :] = hi
+            SL[rows, :] = lo
+            NC[rows, :] = n
 
     def prep_at(at):
         prep(at, GX[at], GL[at])
 
-    def prep_line(b):
-        NC[b] = put((n_lev + b) * blk, CX[b])
-        L0[b] = jnp.transpose(jnp.broadcast_to(CC[b], (blk, blk)))[:, 0:1].astype(F32)
-
-    def slot_of(j):
-        return jnp.where(j == 0, OWN, jnp.where(j == 1, jnp.where(z == 2, 3, 0),
-                         jnp.where(j == 2, jnp.where(z == 1, 2, 0), 3)))
-
-    def unit(j, g):
-        s = slot_of(j)
-        own = s == OWN
-        c = pl.ds(pl.multiple_of(jnp.where(own, 0, n_lev + s) * blk, blk), blk)
-        rows = pl.ds(pl.multiple_of(g * span, span), span)
-        chi, clo = HI[c, :], LO[c, :]
-        hi, lo, lb = HI[rows, :], LO[rows, :], LB[rows, :]
-        dots = nt(chi, hi) + nt(chi, lo) + nt(clo, hi)
-        dist = jnp.maximum(NC[s] + NR[:, rows] - 2.0 * dots, 0.0)
-        kern = jnp.exp(dist * scale)
-        gap = lax.broadcasted_iota(jnp.int32, kern.shape, 1) - lax.broadcasted_iota(jnp.int32, kern.shape, 0)
-        kern = jnp.where(gap == jnp.where(own & (g == 0), 0, n_lev * blk), 0.0, kern)
-        kh, kl = split(kern)
-        PROJ[s] += nn(kh, lb) + nn(kl, lb)
-        t = jnp.sum(kern, axis=0, keepdims=True)
-        w = jnp.where(own, 1.0, 2.0)
-        TOT[...] += w * (t[:, :blk] + t[:, blk:])
-        ROWP[:, rows] += jnp.sum(kern * L0[s], axis=0, keepdims=True)
-
-    def units(j0, j1, g0, g1):
-        def outer(j, _):
-            def inner(g, _):
-                unit(j, g)
-                return 0
-            lax.fori_loop(g0, g1, inner, 0)
-            return 0
-        lax.fori_loop(j0, j1, outer, 0)
-
-    early = jnp.where(z == 0, 1, 4 - z)
-    every = jnp.where(z == 0, 1, 5 - z)
-    NC[OWN] = prep(0, x_ref[...], l_ref[...])
-    L0[OWN] = jnp.zeros((blk, 1), F32)
+    def prep_line(b, j):
+        hi, lo = split(CX[b])
+        rows = slice(j * blk, (j + 1) * blk)
+        SH[rows, :] = hi
+        SL[rows, :] = lo
+        NC[rows, :] = norms(CX[b])
+        L0[rows, :] = jnp.transpose(jnp.broadcast_to(CC[b], (blk, blk)))[:, 0:1].astype(F32)
+
+    def work(j0, j1, *groups):
+        mine = slice(j0 * blk, j1 * blk)
+        n = (j1 - j0) * blk
+        tiles = []
+        for g in groups:
+            rows = slice(g * span, (g + 1) * span)
+            hi = SH[mine, :]
+            d = nt(jnp.concatenate([hi, SL[mine, :]], axis=0), HI[rows, :])
+            tiles.append((g, rows, d[:n] + d[n:] + nt(hi, LO[rows, :])))
+        for g, rows, dots in tiles:
+            dist = jnp.maximum(NC[mine, :] + NR[:, rows] - 2.0 * dots, 0.0)
+            kern = jnp.exp(dist * scale)
+            if j0 == 0:
+                top = kern[:blk]
+                if g == 0:
+                    gap = lax.broadcasted_iota(jnp.int32, top.shape, 1) - lax.broadcasted_iota(jnp.int32, top.shape, 0)
+                    top = jnp.where(gap == 0, 0.0, top)
+                    kern = top if n == blk else jnp.concatenate([top, kern[blk:]], axis=0)
+                t = jnp.sum(top, axis=0, keepdims=True)
+            else:
+                t = jnp.zeros((1, span), F32)
+            kh, kl = split(kern)
+            p = nn(jnp.concatenate([kh, kl], axis=0), LB[rows, :])
+            PROJ[mine, :] += p[:n] + p[n:]
+            rest = kern[blk:] if j0 == 0 else kern
+            if rest.shape[0]:
+                t = t + 2.0 * jnp.sum(rest, axis=0, keepdims=True)
+                line_rows = slice(max(j0, 1) * blk, j1 * blk)
+                ROWP[:, rows] += jnp.sum(rest * L0[line_rows, :], axis=0, keepdims=True)
+            TOT[...] += t[:, :blk] + t[:, blk:]
+
+    prep(0, x_ref[...], l_ref[...])
     xy_wait(1)
     prep_at(1)
-    units(0, 1, 0, 1)
+
+    @at_z(0, 3)
+    def _():
+        work(0, 1, 0)
 
     @at_z(1)
     def _():
@@ -661,25 +667,19 @@
     @at_z(1)
     def _():
         z_pass(0, [3, 4], 1)
-        prep_line(0)
+        prep_line(0, 1)
         z_wait(2, SAM + [4])
-        prep_line(2)
+        prep_line(2, 2)
+        work(0, 3, 0)
+        z_pass(0, LAB, 1)
 
     @at_z(2)
     def _():
         z_pass(3, [3, 4], -1)
         z_start(2, LAB, True, -1)
-        prep_line(3)
+        prep_line(3, 1)
         z_pass(0, [0], 1)
-
-    units(1, early, 0, 1)
-
-    @at_z(1)
-    def _():
-        z_pass(0, LAB, 1)
-
-    @at_z(2)
-    def _():
+        work(0, 2, 0)
         z_pass(0, [1], 1)
         z_pass(3, LAB[:3], -1)
         z_pass(0, [2], 1)
@@ -691,21 +691,37 @@
     xy_start(3, 5, A, k_dev)
     prep_at(2)
     prep_at(3)
-    units(0, early, 1, 2)
+
+    @at_z(0, 3)
+    def _():
+        work(0, 1, 1)
+
+    @at_z(1)
+    def _():
+        work(0, 3, 1)
 
     @at_z(2)
     def _():
+        work(0, 2, 1)
         z_pass(0, [3, 4], 1)
-        prep_line(0)
+        prep_line(0, 2)
 
     xy_wait(4)
     xy_wait(5)
     prep_at(4)
     prep_at(5)
-    units(0, early, 2, 3)
+
+    @at_z(0, 3)
+    def _():
+        work(0, 1, 2)
+
+    @at_z(1)
+    def _():
+        work(0, 3, 2)
 
     @at_z(2)
     def _():
+        work(0, 2, 2)
         z_pass(0, LAB[:2], 1)
 
     for part in (A, B):
@@ -715,11 +731,8 @@
     @at_z(1)
     def _():
         z_wait(3, SAM + [4])
-        prep_line(3)
-
-    @at_z(1, 2)
-    def _():
-        units(early, every, 0, 1)
+        prep_line(3, 3)
+        work(3, 4, 0, 1, 2)
 
     for part in (A, B):
         xy_wait(6, (part,), (L,))
@@ -728,61 +741,73 @@
     @at_z(2)
     def _():
         z_pass(0, LAB[2:], 1)
+        work(2, 3, 0, 1, 2)
 
     @at_z(3)
     def _():
         z_wait(0, SAM + [4])
-        prep_line(0)
+        prep_line(0, 1)
+        work(1, 2, 0, 1, 2)
 
     @at_z(0, 3)
     def _():
         pl.semaphore_wait(line, 1)
 
-    units(early, every, jnp.where(z == 3, 0, 1), 3)
     prep_at(6)
     xy_wait(7)
     for xx, yy, kk in place[1:]:
         signal(here, dev(z, xx, yy, kk))
     prep_at(7)
-    units(0, every, 3, 4)
+    for level in range(nz):
+        @at_z(level)
+        def _():
+            work(0, 1 + len(order[level]), 3)
+
+    def proj(j):
+        return PROJ[j * blk:(j + 1) * blk, :]
 
     none = jnp.zeros((1, 128), F32)
-    own_proof = to_row(PROJ[OWN][:, 0:1])
+    own_proof = to_row(proj(0)[:, 0:1])
     tot = TOT[...]
     for i in range(n_lev):
         S1[i, qr:qr + 1, :] = tot
         S1[i, qr + 1:qr + 2, :] = ROWP[:, i * blk:(i + 1) * blk]
     for b in range(nz + 1):
         S2[b, qr:qr + 1, :] = tot
-        S2[b, qr + 1:qr + 2, :] = to_row(PROJ[b][:, 0:1]) if b in (0, 2, 3) else none
-
-    def quad_of(s, lv):
-        return jnp.sum(lv.astype(F32) * PROJ[s], axis=0, keepdims=True)
-
-    def add(q):
-        for j in range(qr):
-            S2[nz, j:j + 1, :] += q[:, j * 128:(j + 1) * 128]
+        S2[b, qr + 1:qr + 2, :] = none
+    for level in range(1, nz):
+        @at_z(level)
+        def _():
+            for j, b in enumerate(order[level]):
+                S2[b, qr + 1:qr + 2, :] = to_row(proj(j + 1)[:, 0:1])
+
+    def add(w, j, lv):
+        q = w * jnp.sum(lv.astype(F32) * proj(j), axis=0, keepdims=True)
+        for i in range(qr):
+            S2[nz, i:i + 1, :] += q[:, i * 128:(i + 1) * 128]
 
     S2[nz, 0:qr, :] = jnp.zeros((qr, 128), F32)
-    add(quad_of(OWN, l_ref[...]))
+    add(1.0, 0, l_ref[...])
 
     @at_z(3)
     def _():
         z_wait(0, LAB)
 
-    @at_z(1, 2, 3)
-    def _():
-        add(2.0 * quad_of(0, CL[0]))
+    @at_z(1, 3)
+    def _():
+        add(2.0, 1, CL[0])
+
+    @at_z(2)
+    def _():
+        add(2.0, 1, CL[3])
+        add(2.0, 2, CL[0])
 
     @at_z(1)
     def _():
         z_wait(2, LAB)
-        add(2.0 * quad_of(2, CL[2]))
+        add(2.0, 2, CL[2])
         z_wait(3, LAB)
-
-    @at_z(1, 2)
-    def _():
-        add(2.0 * quad_of(3, CL[3]))
+        add(2.0, 3, CL[3])
 
     q = S2[nz, 0:qr, :]
     for i in range(n_lev):
@@ -859,15 +884,17 @@
             pltpu.VMEM((nz, blk, width), F32),
             pltpu.VMEM((nz, blk, perms), i32),
             pltpu.VMEM((nz, 1, blk), i32),
-            pltpu.VMEM(((n_lev + nz) * blk, width), BF16),
-            pltpu.VMEM(((n_lev + nz) * blk, width), BF16),
+            pltpu.VMEM((n_lev * blk, width), BF16),
+            pltpu.VMEM((n_lev * blk, width), BF16),
             pltpu.VMEM((n_lev * blk, perms), BF16),
+            pltpu.VMEM((nz * blk, width), BF16),
+            pltpu.VMEM((nz * blk, width), BF16),
             pltpu.VMEM((1, n_lev * blk), F32),
-            pltpu.VMEM((nz + 1, blk, 1), F32),
-            pltpu.VMEM((nz + 1, blk, 1), F32),
+            pltpu.VMEM((nz * blk, 1), F32),
+            pltpu.VMEM((nz * blk, 1), F32),
             pltpu.VMEM((1, blk), i32),
             pltpu.VMEM((1, n_lev * blk), F32),
-            pltpu.VMEM((nz + 1, blk, perms), F32),
+            pltpu.VMEM((nz * blk, perms), F32),
             pltpu.VMEM((1, blk), F32),
             pltpu.VMEM((n_lev, qr + 2, 128), F32),
             pltpu.VMEM((nz + 1, qr + 2, 128), F32),

time: 34.2 us -> 32.8 us (0.959)
  Pallas kernels: 33.4 us -> 32 us
    pallas_call x1, Pallas kernels: 32 us -> 30.6 us  [line_call(): pl.pallas_call(line_kernel, out_shape=jax.ShapeDtypeStruct((qr + 2, 128),...]
where the time goes in v2:
time: 32.8 us; the launch traced here: 32.6 us
  Pallas kernels  32 us (98%)
  between operations  0.64 us (2%)
    pallas_call x1, Pallas kernels, line_call(): pl.pallas_call(line_kernel, out_shape=jax.ShapeDtypeStruct((qr + 2, 128),...  30.6 us
    pallas_call x1, Pallas kernels, line_call(): pl.pallas_call(functools.partial(finish, blk * slots, perms), out_shape=(...  1.4 us

profile of v2, /device:TPU:0, one launch (start us, length us, event | category | flops | bytes accessed | tf_op | source)
XLA Modules:
  0.0 32.6 jit_solution(17156272713130812014)
XLA Ops:
  0.6 30.6 %shard_map.49.r_ref = f32[4,128]{1,0:T(4,128)} custom-call(f32[128,512]{1,0:T(8,128)} %x_hbm.1, s32[128,256]{1,0:T(8,128)} %l_hbm.1), custom_call_target="tpu_custom_call" | custom-call | tf_op jit(solution)/shard_map/pallas_call | solution.py:874
  31.2 1.4 %shard_map.50 = (f32[2,128]{1,0:T(2,128)}, f32[1,128]{1,0:T(1,128)}, f32[1,1]{1,0:T(1,128)}) custom-call(f32[4,128]{1,0:T(4,128)} %shard_map.49.r_ref), custom_call_target="tpu_custom_call" | custom-call | tf_op jit(solution)/shard_map/pallas_call | solution.py:916

commit v3 on v2

--- a/solution.py
+++ b/solution.py
@@ -446,7 +446,7 @@
 
 
 def line_kernel(x_hbm, l_hbm, out_ref, x_ref, l_ref, GX, GL, CX, CL, CC, HI, LO, LB, SH, SL, NR, NC, L0, OWN0,
-                ROWP, PROJ, TOT, S1, S2, R1, in_sem, xy_send, xy_recv, z_send, z_recv, m_send, m_recv, line, here):
+                ROWP, PROJ, TOT, S1, R1, in_sem, xy_send, xy_recv, z_send, z_recv, m_send, m_recv, line, here):
     blk, width = x_ref.shape
     perms = l_ref.shape[1]
     nx, ny, nk, nz, n_lev = 2, 2, 2, 4, 8
@@ -689,6 +689,12 @@
     xy_start(2, 4, B, k_dev)
     xy_wait(3, (A,))
     xy_start(3, 5, A, k_dev)
+
+    @at_z(0, 3)
+    def _():
+        pl.semaphore_wait(line, 1)
+
+    signal(here.at[0], k_dev)
     prep_at(2)
     prep_at(3)
 
@@ -708,6 +714,8 @@
 
     xy_wait(4)
     xy_wait(5)
+    pl.semaphore_wait(here.at[0], 1)
+    signal(here.at[1], x_dev)
     prep_at(4)
     prep_at(5)
 
@@ -727,6 +735,8 @@
     for part in (A, B):
         xy_wait(6, (part,), (X,))
         xy_start(6, 7, part, k_dev, (X,))
+    pl.semaphore_wait(here.at[1], 1)
+    signal(here.at[2], y_dev)
 
     @at_z(1)
     def _():
@@ -749,14 +759,8 @@
         prep_line(0, 1)
         work(1, 2, 0, 1, 2)
 
-    @at_z(0, 3)
-    def _():
-        pl.semaphore_wait(line, 1)
-
     prep_at(6)
     xy_wait(7)
-    for xx, yy, kk in place[1:]:
-        signal(here, dev(z, xx, yy, kk))
     prep_at(7)
     for level in range(nz):
         @at_z(level)
@@ -773,20 +777,20 @@
         S1[i, qr:qr + 1, :] = tot
         S1[i, qr + 1:qr + 2, :] = ROWP[:, i * blk:(i + 1) * blk]
     for b in range(nz + 1):
-        S2[b, qr:qr + 1, :] = tot
-        S2[b, qr + 1:qr + 2, :] = none
+        S1[n_lev + b, qr:qr + 1, :] = tot
+        S1[n_lev + b, qr + 1:qr + 2, :] = none
     for level in range(1, nz):
         @at_z(level)
         def _():
             for j, b in enumerate(order[level]):
-                S2[b, qr + 1:qr + 2, :] = to_row(proj(j + 1)[:, 0:1])
+                S1[n_lev + b, qr + 1:qr + 2, :] = to_row(proj(j + 1)[:, 0:1])
 
     def add(w, j, lv):
         q = w * jnp.sum(lv.astype(F32) * proj(j), axis=0, keepdims=True)
         for i in range(qr):
-            S2[nz, i:i + 1, :] += q[:, i * 128:(i + 1) * 128]
-
-    S2[nz, 0:qr, :] = jnp.zeros((qr, 128), F32)
+            S1[n_lev + nz, i:i + 1, :] += q[:, i * 128:(i + 1) * 128]
+
+    S1[n_lev + nz, 0:qr, :] = jnp.zeros((qr, 128), F32)
     add(1.0, 0, l_ref[...])
 
     @at_z(3)
@@ -809,27 +813,31 @@
         z_wait(3, LAB)
         add(2.0, 3, CL[3])
 
-    q = S2[nz, 0:qr, :]
+    q = S1[n_lev + nz, 0:qr, :]
     for i in range(n_lev):
         S1[i, 0:qr, :] = q
     for b in range(nz):
-        S2[b, 0:qr, :] = q
+        S1[n_lev + b, 0:qr, :] = q
     index = z * n_lev + x * 4 + col
-    pl.semaphore_wait(here, n_lev - 1)
-
-    def m_copy(dz, i, incoming):
-        b = (z + dz) % nz
-        xx, yy, kk = place[i]
-        src = S1.at[i] if dz == 0 else (S2.at[b] if i == 0 else S2.at[nz])
-        slot = b * n_lev + xx * 4 + yy * nk + kk if incoming else index
-        return remote(src, R1.at[slot], m_send.at[dz * n_lev + i], m_recv.at[slot], dev(b, xx, yy, kk))
-
-    pairs = [(dz, i) for dz in reversed(range(nz)) for i in range(n_lev) if dz + i > 0]
-    for dz, i in pairs:
-        m_copy(dz, i, False).start()
+    pl.semaphore_wait(here.at[2], 1)
+
+    def m_copy(t, incoming):
+        tz, tx, ty, tk = t // n_lev, t // 4 % nx, t // nk % ny, t % nk
+        dx, dy, dk = jnp.where(tx == x, 0, 1), jnp.where(ty == y, 0, 1), jnp.where(tk == core, 0, 1)
+        i = jnp.where(dk == 0, 2 * dx + 3 * dy + dx * dy, jnp.where(dx + dy == 0, 1, 3 + dx + 2 * dy + dx * dy))
+        n = jnp.where(tz == z, i, n_lev + jnp.where(i == 0, tz, nz))
+        return remote(S1.at[n], R1.at[t if incoming else index], m_send.at[t], m_recv.at[t if incoming else index],
+                      dev(tz, tx, ty, tk))
+
+    def others(act):
+        for t in range(nz * n_lev):
+            @pl.when(t != index)
+            def _():
+                act(t)
+
+    others(lambda t: m_copy(t, False).start())
     R1[index] = S1[0]
-    for dz, i in pairs:
-        m_copy(dz, i, True).wait_recv()
+    others(lambda t: m_copy(t, True).wait_recv())
     done = R1[0]
     for i in range(1, nz * n_lev):
         done = done + R1[i]
@@ -843,8 +851,7 @@
         def _():
             for p in SAM + [4] + LAB:
                 z_copy(b, p, False, here_dev).wait_send()
-    for dz, i in pairs:
-        m_copy(dz, i, False).wait_send()
+    others(lambda t: m_copy(t, False).wait_send())
 
 
 def finish(rows, perms, r_ref, stat_ref, proof_ref, p_ref):
@@ -896,8 +903,7 @@
             pltpu.VMEM((1, n_lev * blk), F32),
             pltpu.VMEM((nz * blk, perms), F32),
             pltpu.VMEM((1, blk), F32),
-            pltpu.VMEM((n_lev, qr + 2, 128), F32),
-            pltpu.VMEM((nz + 1, qr + 2, 128), F32),
+            pltpu.VMEM((n_lev + nz + 1, qr + 2, 128), F32),
             pltpu.VMEM((slots, qr + 2, 128), F32),
             dma((2,)),
             dma((n_lev, 4)),
@@ -907,7 +913,7 @@
             dma((slots,)),
             dma((slots,)),
             pltpu.SemaphoreType.REGULAR,
-            pltpu.SemaphoreType.REGULAR,
+            pltpu.SemaphoreType.REGULAR((3,)),
         ],
         compiler_params=pltpu.CompilerParams(
             collective_id=1, has_side_effects=True, vmem_limit_bytes=LIMIT

time: 32.8 us -> 32.3 us (0.985)
  Pallas kernels: 32 us -> 31.5 us
    pallas_call x1, Pallas kernels: 30.6 us -> 30.1 us  [line_call(): pl.pallas_call(line_kernel, out_shape=jax.ShapeDtypeStruct((qr + 2, 128),...]
where the time goes in v3:
time: 32.3 us; the launch traced here: 32.2 us
  Pallas kernels  31.5 us (98%)
  between operations  0.64 us (2%)
    pallas_call x1, Pallas kernels, line_call(): pl.pallas_call(line_kernel, out_shape=jax.ShapeDtypeStruct((qr + 2, 128),...  30.1 us
    pallas_call x1, Pallas kernels, line_call(): pl.pallas_call(functools.partial(finish, blk * slots, perms), out_shape=(...  1.4 us

profile of v3, /device:TPU:0, one launch (start us, length us, event | category | flops | bytes accessed | tf_op | source)
XLA Modules:
  0.0 32.2 jit_solution(18096825554412267949)
XLA Ops:
  0.6 30.1 %shard_map.49.r_ref = f32[4,128]{1,0:T(4,128)} custom-call(f32[128,512]{1,0:T(8,128)} %x_hbm.1, s32[128,256]{1,0:T(8,128)} %l_hbm.1), custom_call_target="tpu_custom_call" | custom-call | tf_op jit(solution)/shard_map/pallas_call | solution.py:881
  30.8 1.4 %shard_map.50 = (f32[2,128]{1,0:T(2,128)}, f32[1,128]{1,0:T(1,128)}, f32[1,1]{1,0:T(1,128)}) custom-call(f32[4,128]{1,0:T(4,128)} %shard_map.49.r_ref), custom_call_target="tpu_custom_call" | custom-call | tf_op jit(solution)/shard_map/pallas_call | solution.py:922

commit v4 on v3

--- a/solution.py
+++ b/solution.py
@@ -454,7 +454,7 @@
     z, x = row // nx, row % nx
     y, core = col // nk, col % nk
     qr = perms // 128
-    A, B = 0, 1
+    A, B, ALL = 0, 1, 2
 
     def dev(zz, xx, yy, kk):
         return (zz * nx + xx, yy * nk + kk)
@@ -497,10 +497,10 @@
     half = blk // 2
 
     def xy_copy(src, dst, part, i, to):
-        r = pl.ds(part * half, half)
+        r = pl.ds(part * half, half) if part < 2 else pl.ds(0, blk)
         mine, buf = ((x_ref, GX), (l_ref, GL))[i]
         s = mine.at[r] if src == 0 else buf.at[src, r]
-        n = part * 2 + i
+        n = part % 2 * 2 + i
         return remote(s, buf.at[dst, r], xy_send.at[dst, n], xy_recv.at[dst, n], to)
 
     sent = []
@@ -520,25 +520,33 @@
     piece = blk // 4
     SAM, LAB = [0, 1, 2, 3], [5, 6, 7, 8]
 
+    EACH = {p: (p % 5, p % 5 + 1) for p in SAM + LAB}
+    WHOLE = {3: (0, 4), 8: (0, 4)}
+    CUTS = {0: EACH, 2: WHOLE, 3: {1: (0, 2), 3: (2, 4), 8: (0, 4)}}
+
+    def held(b, ps):
+        return [p for p in ps if p == 4 or p in CUTS[b]]
+
     def z_copy(b, p, own, to):
         if p == 4:
             src, dst = (OWN0 if own else CC.at[b]), CC.at[b]
         else:
-            r = pl.ds((p if p < 4 else p - 5) * piece, piece)
+            first, end = CUTS[b][p]
+            r = pl.ds(first * piece, (end - first) * piece)
             mine, buf = (x_ref, CX) if p < 4 else (l_ref, CL)
             src, dst = (mine.at[r] if own else buf.at[b, r]), buf.at[b, r]
         return remote(src, dst, z_send.at[b, p], z_recv.at[b, p], to)
 
     def z_start(b, ps, own, step):
-        for p in ps:
+        for p in held(b, ps):
             z_copy(b, p, own, dev(z + step, x, y, core)).start()
 
     def z_wait(b, ps):
-        for p in ps:
+        for p in held(b, ps):
             z_copy(b, p, False, here_dev).wait_recv()
 
     def z_pass(b, ps, step):
-        for p in ps:
+        for p in held(b, ps):
             z_wait(b, [p])
             z_start(b, [p], False, step)
 
@@ -569,8 +577,7 @@
     xy_start(0, 3, B, y_dev)
     xy_start(0, 2, B, x_dev)
     xy_start(0, 3, A, y_dev)
-    xy_start(0, 1, A, k_dev)
-    xy_start(0, 1, B, k_dev)
+    xy_start(0, 1, ALL, k_dev)
 
     scale = -1.0 / (2.0 * width)
     span = nk * blk
@@ -636,7 +643,7 @@
             TOT[...] += t[:, :blk] + t[:, blk:]
 
     prep(0, x_ref[...], l_ref[...])
-    xy_wait(1)
+    xy_wait(1, (ALL,))
     prep_at(1)
 
     @at_z(0, 3)
@@ -732,9 +739,8 @@
         work(0, 2, 2)
         z_pass(0, LAB[:2], 1)
 
-    for part in (A, B):
-        xy_wait(6, (part,), (X,))
-        xy_start(6, 7, part, k_dev, (X,))
+    xy_wait(6, (A, B), (X,))
+    xy_start(6, 7, ALL, k_dev, (X,))
     pl.semaphore_wait(here.at[1], 1)
     signal(here.at[2], y_dev)
 
@@ -744,14 +750,15 @@
         prep_line(3, 3)
         work(3, 4, 0, 1, 2)
 
-    for part in (A, B):
-        xy_wait(6, (part,), (L,))
-        xy_start(6, 7, part, k_dev, (L,))
+    xy_wait(6, (A, B), (L,))
+    xy_start(6, 7, ALL, k_dev, (L,))
 
     @at_z(2)
     def _():
         z_pass(0, LAB[2:], 1)
         work(2, 3, 0, 1, 2)
+
+    prep_at(6)
 
     @at_z(3)
     def _():
@@ -759,8 +766,7 @@
         prep_line(0, 1)
         work(1, 2, 0, 1, 2)
 
-    prep_at(6)
-    xy_wait(7)
+    xy_wait(7, (ALL,))
     prep_at(7)
     for level in range(nz):
         @at_z(level)
@@ -837,21 +843,24 @@
 
     others(lambda t: m_copy(t, False).start())
     R1[index] = S1[0]
-    others(lambda t: m_copy(t, True).wait_recv())
-    done = R1[0]
-    for i in range(1, nz * n_lev):
-        done = done + R1[i]
-    out_ref[0:qr + 1, :] = done[0:qr + 1, :]
-    out_ref[qr + 1:qr + 2, :] = done[qr + 1:qr + 2, :] + own_proof
 
     for c in sent:
         c.wait_send()
     for at, b in ((0, 0), (1, 0), (2, 0), (2, 2), (2, 3), (3, 3)):
         @at_z(at)
         def _():
-            for p in SAM + [4] + LAB:
+            for p in held(b, SAM + [4] + LAB):
                 z_copy(b, p, False, here_dev).wait_send()
+
     others(lambda t: m_copy(t, False).wait_send())
+    done = jnp.zeros((qr + 2, 128), F32)
+    for t in range(nz * n_lev):
+        @pl.when(t != index)
+        def _():
+            m_copy(t, True).wait_recv()
+        done = done + R1[t]
+    out_ref[0:qr + 1, :] = done[0:qr + 1, :]
+    out_ref[qr + 1:qr + 2, :] = done[qr + 1:qr + 2, :] + own_proof
 
 
 def finish(rows, perms, r_ref, stat_ref, proof_ref, p_ref):

time: 32.3 us -> 32.1 us (level)
  no operation moved by 1% of the time
where the time goes in v4:
time: 32.1 us; the launch traced here: 32 us
  Pallas kernels  31.3 us (98%)
  between operations  0.64 us (2%)
    pallas_call x1, Pallas kernels, line_call(): pl.pallas_call(line_kernel, out_shape=jax.ShapeDtypeStruct((qr + 2, 128),...  29.9 us
    pallas_call x1, Pallas kernels, line_call(): pl.pallas_call(functools.partial(finish, blk * slots, perms), out_shape=(...  1.4 us

profile of v4, /device:TPU:0, one launch (start us, length us, event | category | flops | bytes accessed | tf_op | source)
XLA Modules:
  0.0 32.0 jit_solution(6197510011904504285)
XLA Ops:
  0.6 29.9 %shard_map.49.r_ref = f32[4,128]{1,0:T(4,128)} custom-call(f32[128,512]{1,0:T(8,128)} %x_hbm.1, s32[128,256]{1,0:T(8,128)} %l_hbm.1), custom_call_target="tpu_custom_call" | custom-call | tf_op jit(solution)/shard_map/pallas_call | solution.py:890
  30.6 1.4 %shard_map.50 = (f32[2,128]{1,0:T(2,128)}, f32[1,128]{1,0:T(1,128)}, f32[1,1]{1,0:T(1,128)}) custom-call(f32[4,128]{1,0:T(4,128)} %shard_map.49.r_ref), custom_call_target="tpu_custom_call" | custom-call | tf_op jit(solution)/shard_map/pallas_call | solution.py:931

commit v5 on v4

--- a/solution.py
+++ b/solution.py
@@ -478,11 +478,11 @@
     for to in (x_dev, y_dev, k_dev):
         signal(barrier, to)
 
-    @pl.when(z > 0)
-    def _():
-        signal(barrier, dev(z - 1, x, y, core))
-
-    @pl.when(z < nz - 1)
+    @pl.when(z == 1)
+    def _():
+        signal(barrier, dev(0, x, y, core))
+
+    @pl.when((z == 1) | (z == 2))
     def _():
         signal(barrier, dev(z + 1, x, y, core))
 
@@ -492,7 +492,7 @@
     for c in reversed(loads):
         c.wait()
     OWN0[...] = to_row(l_ref[:, 0:1].astype(F32)).astype(jnp.int32)
-    pl.semaphore_wait(barrier, 3 + jnp.where(z > 0, 1, 0) + jnp.where(z < nz - 1, 1, 0))
+    pl.semaphore_wait(barrier, jnp.where(z == 1, 3, 4))
 
     half = blk // 2
 
@@ -559,18 +559,15 @@
     @at_z(0)
     def _():
         z_start(0, SAM + [4] + LAB, True, 1)
+        signal(line, dev(1, x, y, core))
 
     @at_z(2)
     def _():
         z_start(2, SAM + [4], True, -1)
-        signal(line, dev(1, x, y, core))
 
     @at_z(3)
     def _():
         z_start(3, SAM + [4] + LAB, True, -1)
-
-    @at_z(1)
-    def _():
         signal(line, dev(2, x, y, core))
 
     xy_start(0, 2, A, x_dev)
@@ -643,6 +640,12 @@
             TOT[...] += t[:, :blk] + t[:, blk:]
 
     prep(0, x_ref[...], l_ref[...])
+
+    @at_z(2)
+    def _():
+        pl.semaphore_wait(line, 1)
+        signal(line, dev(1, x, y, core))
+
     xy_wait(1, (ALL,))
     prep_at(1)
 
@@ -652,10 +655,10 @@
 
     @at_z(1)
     def _():
-        z_pass(0, [0, 1], 1)
-        pl.semaphore_wait(line, 1)
+        pl.semaphore_wait(line, 2)
         signal(line, dev(0, x, y, core))
-        z_pass(0, [2], 1)
+        signal(line, dev(2, x, y, core))
+        z_pass(0, [0, 1, 2], 1)
 
     @at_z(2)
     def _():

time: 32.1 us -> 32 us (level)
  no operation moved by 1% of the time
where the time goes in v5:
time: 32 us; the launch traced here: 31.8 us
  Pallas kernels  31.2 us (98%)
  between operations  0.64 us (2%)
    pallas_call x1, Pallas kernels, line_call(): pl.pallas_call(line_kernel, out_shape=jax.ShapeDtypeStruct((qr + 2, 128),...  29.8 us
    pallas_call x1, Pallas kernels, line_call(): pl.pallas_call(functools.partial(finish, blk * slots, perms), out_shape=(...  1.4 us

profile of v5, /device:TPU:0, one launch (start us, length us, event | category | flops | bytes accessed | tf_op | source)
XLA Modules:
  0.0 31.8 jit_solution(7238650541740791208)
XLA Ops:
  0.6 29.8 %shard_map.49.r_ref = f32[4,128]{1,0:T(4,128)} custom-call(f32[128,512]{1,0:T(8,128)} %x_hbm.1, s32[128,256]{1,0:T(8,128)} %l_hbm.1), custom_call_target="tpu_custom_call" | custom-call | tf_op jit(solution)/shard_map/pallas_call | solution.py:893
  30.4 1.4 %shard_map.50 = (f32[2,128]{1,0:T(2,128)}, f32[1,128]{1,0:T(1,128)}, f32[1,1]{1,0:T(1,128)}) custom-call(f32[4,128]{1,0:T(4,128)} %shard_map.49.r_ref), custom_call_target="tpu_custom_call" | custom-call | tf_op jit(solution)/shard_map/pallas_call | solution.py:934
